TPU v7x, 32 devices: a whole 2x2x4 slice. The times are simulated.
32 devices in a mesh: gx: 8 (over y, x, core), gy: 4 (over z).
Axes of the slice: x: 2, y: 2, z: 4, core: 2. Of those that a mesh axis runs over, the one named last changes fastest.
Arguments:
- date_key: int32 [393216], P(('gx', 'gy')), may hold values from 0 to 4095
- store_key: int32 [393216], P(('gx', 'gy')), may hold values from 0 to 65535
- product_key: int32 [393216], P(('gx', 'gy')), may hold values from 0 to 1048575
- revenue: bfloat16 [393216], P(('gx', 'gy')), may hold values from -0.59765625 to 0.59765625
- row_counts: int32 [32], P(('gx', 'gy')), may hold values from 1 to 12288, 245760 in all
- date_years: int32 [512], P('gx'), may hold values from -2147483648 to 2147483646
- date_flags: int32 [128], P('gx'), may hold values from -2147483648 to 2147483646
- store_flags: int32 [2048], P('gx'), may hold values from -2147483648 to 2147483646
- product_flags: int32 [32768], P('gx'), may hold values from -2147483648 to 2147483646
- brand_words: int32 [349568], P('gx'), may hold values from 0 to 1073741823
Outputs:
- revenue_groups: float32 [16, 1024], replicated
Inputs may be any that keep to these rules, and one draw needn't show every extreme that they name: Rows d * 12288 to d * 12288 + row_counts[d] - 1 of the fact arrays are live; the largest count equals 12288. `date_years`: date k's year code is in bits 4 * (k % 8) of word k // 8. `date_flags`: bit k % 32 of word k // 32 is the flag of row k. `store_flags`: bit k % 32 of word k // 32 is the flag of row k. `product_flags`: bit k % 32 of word k // 32 is the flag of row k. `brand_words`: product with shard o and local index l holds its brand code in bits 10 * (l % 3) of word o * 43696 + l // 3; words past a shard's products are unused.
All inputs are finite; a program needn't handle non-finite values. No bound on the sum of `row_counts` on one device may be relied on, other than what follows from the above.
Results may differ from a plain program's by a relative error of at most 0.0003.
Values sent between devices are 32-bit elements; how exact they have to be, the bound alone decides.
A program may use at most 64 MiB of HBM per device.

v0:
```python
import jax
import jax.numpy as jnp
from jax import lax
from jax.sharding import PartitionSpec as P

BRANDS = 1024
YEARS = 16


def pick_bits(packed, position, width_bits):
    per_word = 32 // width_bits
    chosen = packed[position // per_word]
    shifted = jnp.right_shift(chosen, position % per_word * width_bits)
    return jnp.bitwise_and(shifted, (1 << width_bits) - 1)


def shards(
    date_key,
    store_key,
    product_key,
    revenue,
    row_counts,
    date_years,
    date_flags,
    store_flags,
    product_flags,
    brand_words,
):
    flag_shard = product_flags.shape[0]
    brand_shard = brand_words.shape[0]
    prod_shard = flag_shard * 32
    year_words, date_bits, store_bits, product_bits, brand_table = (
        lax.all_gather(date_years, "gx", axis=0, tiled=True),
        lax.all_gather(date_flags, "gx", axis=0, tiled=True),
        lax.all_gather(store_flags, "gx", axis=0, tiled=True),
        lax.all_gather(product_flags, "gx", axis=0, tiled=True),
        lax.all_gather(brand_words, "gx", axis=0, tiled=True),
    )

    def brand_place(owner_idx, word_idx):
        return owner_idx * brand_shard + word_idx

    def flag_place(owner_idx, word_idx):
        return owner_idx * flag_shard + word_idx

    block_rows = min(4096, date_key.shape[0])
    row_count = row_counts[0]
    block_total = (row_count + block_rows - 1) // block_rows
    high_groups = YEARS * BRANDS // 128

    def add_block(block_idx, totals):
        first_row = block_idx * block_rows
        date_block = lax.dynamic_slice_in_dim(date_key, first_row, block_rows, 0)
        store_block = lax.dynamic_slice_in_dim(store_key, first_row, block_rows, 0)
        product_block = lax.dynamic_slice_in_dim(product_key, first_row, block_rows, 0)
        money_block = lax.dynamic_slice_in_dim(revenue, first_row, block_rows, 0)
        live_rows = first_row + lax.iota(jnp.int32, block_rows) < row_count
        year_code = pick_bits(year_words, date_block, 4)
        owner_idx = product_block // prod_shard
        local_idx = product_block % prod_shard
        flag_word = product_bits[flag_place(owner_idx, local_idx // 32)]
        product_pass = jnp.bitwise_and(jnp.right_shift(flag_word, local_idx % 32), 1)
        passed = (
            pick_bits(date_bits, date_block, 1)
            * pick_bits(store_bits, store_block, 1)
            * product_pass
        )
        word_val = brand_table[brand_place(owner_idx, local_idx // 3)]
        brand_code = jnp.bitwise_and(jnp.right_shift(word_val, local_idx % 3 * 10), 1023)
        kept_rows = live_rows & (passed == 1)
        amount = jnp.where(kept_rows, money_block, jnp.zeros_like(money_block))
        high_row = year_code * (BRANDS // 128) + brand_code // 128
        weighted = jnp.where(
            lax.iota(jnp.int32, high_groups)[:, None] == high_row[None, :],
            amount[None, :],
            jnp.zeros((), jnp.bfloat16),
        )
        low_hot = (lax.iota(jnp.int32, 128)[:, None] == (brand_code % 128)[None, :]).astype(
            jnp.bfloat16
        )
        return totals + lax.dot_general(
            weighted, low_hot, (((1,), (1,)), ((), ())), preferred_element_type=jnp.float32
        )

    totals = lax.fori_loop(0, block_total, add_block, jnp.zeros((high_groups, 128), jnp.float32))
    group_sums = totals.reshape(YEARS, BRANDS)
    result = lax.psum(group_sums, ("gx", "gy"))
    return result


def solution(mesh):
    placed = (
        P(("gx", "gy")),
        P(("gx", "gy")),
        P(("gx", "gy")),
        P(("gx", "gy")),
        P(("gx", "gy")),
        P("gx"),
        P("gx"),
        P("gx"),
        P("gx"),
        P("gx"),
    )
    return jax.shard_map(shards, mesh=mesh, in_specs=placed, out_specs=P(), check_vma=False)
```

profile of v0, /device:TPU:0, one launch (start us, length us, event | category | flops | bytes accessed | tf_op | source)
XLA Modules:
  0.0 642.2 jit_solution(12886607325947073091)
XLA Ops:
  6.5 1.3 dynamic-slice
  8.5 0.1 broadcast.223
  8.6 1.3 dynamic-update-slice.1
  9.9 1.1 copy-done
  11.0 0.0 all-reduce.9.cloned.1.call-update
  11.0 0.0 all-reduce.7.cloned.1.call-start
  13.0 0.2 dynamic-update-slice
  13.3 0.2 dynamic-update-slice.2
  13.5 9.6 %all-reduce.3 = (s32[512]{0:T(512)S(1)}, s32[128]{0:T(128)S(1)}) all-reduce(s32[512]{0:T(512)S(1)} %dynamic-update-slice, s32[128]{0:T(128)S(1)} %dynamic-update-slice.2), channel_id=1, replica_groups=mesh['gx'=8,'gy'=4] {'gx'}, use_global_device_ids=true, to_apply=%add | all-reduce | flops 640 | bytes 5120
  23.1 8.2 %all-gather = s32[8,1,256]{2,1,0:T(1,128)S(1)} all-gather(s32[1,1,256]{2,1,0:T(1,128)S(1)} %bitcast.8), channel_id=1, replica_groups=mesh['gx'=8,'gy'=4] {'gx'}, dimensions={0}, use_global_device_ids=true | all-gather | bytes 9216 | tf_op jit(solution)/shard_map/all_gather | solution.py:35
  31.2 8.9 %all_gather.19 = s32[32768]{0:T(1024)S(1)} all-gather(s32[4096]{0:T(1024)S(1)} %copy-done.5), channel_id=1, replica_groups=mesh['gx'=8,'gy'=4] {'gx'}, dimensions={0}, use_global_device_ids=true | all-gather | bytes 147456 | tf_op jit(solution)/shard_map/all_gather | solution.py:36
  40.2 31.9 %all-reduce.9.cloned.1.call-done = s32[349568]{0:T(1024)} async-done(((s32[349568]{0:T(1024)}), s32[349568]{0:T(1024)}) %all-reduce.9.cloned.1.call-update) | async-done | bytes 1398288
  72.1 147.4 %while.13 = (s32[]{:T(128)}, f32[128,128]{1,0:T(8,128)S(1)}, s32[]{:T(128)}, s32[12288]{0:T(1024)S(1)}, s32[512]{0:T(512)S(1)}, /*index=5*/s32[12288]{0:T(1024)S...) while((s32[]{:T(128)}, f32[128,128]{1,0:T(8,128)S(1)}, ...), condition=%wide.region_1.2_spmd, body=%wide.region_0.1_spmd.sunk | while | flops 136749056 | bytes 860395 | solution.py:85
  72.3 48.4 %gather_fusion.1 = s32[4096]{0:T(1024)S(1)} fusion(s32[349568]{0:T(1024)} %get-tuple-element.421, s32[4096]{0:T(1024)S(1)} %fusion.57), kind=kCustom, calls=%fused_computation.1.clone.1 | custom fusion | bytes 49152 | tf_op jit(solution)/shard_map/while/body/gather | solution.py:68
  120.8 25.9 %gather_fusion = s32[4096]{0:T(1024)S(1)} fusion(s32[512]{0:T(512)S(1)} %get-tuple-element.419, s32[4096]{0:T(1024)S(1)} %fusion.55), kind=kCustom, calls=%fused_computation.clone.1 | custom fusion | bytes 49152 | tf_op jit(solution)/shard_map/while/body/gather | solution.py:12
  146.7 0.1 fusion.58
  146.7 23.0 %gather_fusion.3 = s32[4096]{0:T(1024)S(1)} fusion(s32[2048]{0:T(1024)S(1)} %get-tuple-element.425, s32[4096]{0:T(1024)S(1)} %get-tuple-element.378), kind=kCustom, calls=%fused_computation.3.clone.1 | custom fusion | bytes 49152 | tf_op jit(solution)/shard_map/while/body/gather | solution.py:12
  169.8 23.0 %gather_fusion.2 = s32[4096]{0:T(1024)S(1)} fusion(s32[32768]{0:T(1024)S(1)} %get-tuple-element.426, s32[4096]{0:T(1024)S(1)} %get-tuple-element.377), kind=kCustom, calls=%fused_computation.4.clone.1 | custom fusion | bytes 49152 | tf_op jit(solution)/shard_map/while/body/gather | solution.py:61
  192.8 24.7 %gather_fusion.4 = s32[4096]{0:T(1024)S(1)} fusion(s32[128]{0:T(128)S(1)} %get-tuple-element.423, s32[4096]{0:T(1024)S(1)} %get-tuple-element.379), kind=kCustom, calls=%fused_computation.2.clone.1 | custom fusion | bytes 49152 | tf_op jit(solution)/shard_map/while/body/gather | solution.py:12
  217.5 1.4 fusion.59
  218.9 0.7 fusion.60
  219.6 0.6 reshape.6
  220.3 413.7 %all-reduce.7.cloned.1.call-done = f32[16,1024]{1,0:T(8,128)} async-done(((f32[16,1024]{1,0:T(8,128)}), f32[16,1024]{1,0:T(8,128)}) %all-reduce.7.cloned.1.call-update) | async-done | bytes 65552 | tf_op jit(solution)/shard_map/psum | solution.py:87
  633.9 1.5 copy.23
  (26 shorter events, 0.2 us)
Async XLA Ops:
  6.5 2.1 copy-start.4
  6.5 65.6 %all-reduce.9.cloned.1.call-start = ((), (), s32[]{:S(2)}) async-start(), calls=%async_computation.1 | async-start | bytes 2801664
  8.5 4.6 copy-start.7
  8.5 4.8 copy-start.8
  8.5 14.6 %copy-start.6 = (s32[256]{0:T(256)S(1)}, s32[256]{0:T(256)}, u32[]{:S(2)}) copy-start(s32[256]{0:T(256)} %param.19) | copy-start | bytes 3076
  8.5 22.8 %copy-start.5 = (s32[4096]{0:T(1024)S(1)}, s32[4096]{0:T(1024)}, u32[]{:S(2)}) copy-start(s32[4096]{0:T(1024)} %param.20) | copy-start | bytes 49156
  8.5 63.6 %copy-start.1 = (s32[12288]{0:T(1024)S(1)}, s32[12288]{0:T(1024)}, u32[]{:S(2)}) copy-start(s32[12288]{0:T(1024)} %param.12) | copy-start | bytes 147460
  8.5 63.6 %copy-start.2 = (s32[12288]{0:T(1024)S(1)}, s32[12288]{0:T(1024)}, u32[]{:S(2)}) copy-start(s32[12288]{0:T(1024)} %param.14) | copy-start | bytes 147460
  8.5 63.6 %copy-start.3 = (s32[12288]{0:T(1024)S(1)}, s32[12288]{0:T(1024)}, u32[]{:S(2)}) copy-start(s32[12288]{0:T(1024)} %param.13) | copy-start | bytes 147460
  9.9 1.1 copy-start
  11.0 622.9 %all-reduce.7.cloned.1.call-start = ((), (), s32[]{:S(2)}) async-start(), calls=%async_computation | async-start | bytes 131072 | tf_op jit(solution)/shard_map/psum | solution.py:87
Sparse Core Ops, SparseCore 0:
  11.2 60.9 all-reduce.8
  220.4 413.4 all-reduce.6
where the time goes:
time: 649 us; the launch traced here: 642 us
  waiting for transfers between devices  446 us (69%)
  local copies, waits for them, and re-layouts  151 us (23%)
  blocking collectives  26.7 us (4%)
  between operations  16.1 us (2%)
    psum x1, waiting for transfers between devices, shards(): result = lax.psum(group_sums, ('gx', 'gy'))  414 us
    gather x3, local copies, waits for them, and re-layouts, pick_bits(): chosen = packed[position // per_word]  73.6 us
    gather x1, local copies, waits for them, and re-layouts, add_block(): word_val = brand_table[brand_place(owner_idx, local_idx // 3)]  48.4 us
    unnamed x3, waiting for transfers between devices  32 us
    gather x1, local copies, waits for them, and re-layouts, add_block(): flag_word = product_bits[flag_place(owner_idx, local_idx // 32)]  23 us
  transfers between devices with their start and end apart: 2, of which 2 were waited for; matrix products, arithmetic and copies ran while one was open for 0% of the time, Pallas kernels for 0%

commit v1 on v0

v1 whole, which is shorter than its diff:
```python
import functools

import jax
import jax.numpy as jnp
from jax import lax
from jax.experimental import pallas as pl
from jax.experimental.pallas import tpu as pltpu
from jax.sharding import PartitionSpec as P

BRANDS = 1024
YEARS = 16
LANES = 128
GROUP = 4
MESH = pl.DeviceIdType.MESH
VMEM = pl.BlockSpec(memory_space=pltpu.VMEM)
SMEM = pl.BlockSpec(memory_space=pltpu.SMEM)


def up(count, unit):
    return (count + unit - 1) // unit * unit


def flip(me, mask):
    out, bit = me, 1
    while bit <= mask:
        if mask & bit:
            out = out + bit * (1 - 2 * ((me // bit) % 2))
        bit *= 2
    return out


def spread_kernel(n, x_ref, o_ref, own_sem, send_sem, recv_sem):
    me = lax.axis_index("gx")
    half = x_ref.shape[0] // 2
    bits = n.bit_length() - 1
    rising = [1 << b for b in range(1, bits)]
    orders = (rising + [1], rising[::-1] + [1])
    barrier = pltpu.get_barrier_semaphore()
    for b in range(bits):
        pl.semaphore_signal(barrier, inc=1, device_id={"gx": flip(me, 1 << b)}, device_id_type=MESH)
    own = pltpu.make_async_copy(x_ref, o_ref.at[me], own_sem)
    own.start()
    pl.semaphore_wait(barrier, bits)

    def copy(h, mask, step):
        rows = pl.ds(h * half, half)
        slot = flip(me, mask)
        src = x_ref.at[rows] if mask == 0 else o_ref.at[slot, rows]
        return pltpu.make_async_remote_copy(
            src_ref=src,
            dst_ref=o_ref.at[slot, rows],
            send_sem=send_sem.at[h, mask + step],
            recv_sem=recv_sem.at[h, mask + step],
            device_id={"gx": flip(me, step)},
            device_id_type=MESH,
        )

    sent = []
    for h in range(2):
        for step in orders[h]:
            c = copy(h, 0, step)
            c.start()
            sent.append(c)
    arrivals = []
    for h in range(2):
        have = [0]
        listed = []
        for step in orders[h]:
            fresh = [m + step for m in have]
            listed += [(m, step) for m in fresh]
            have += fresh
        arrivals.append(listed)
    for pair in zip(*arrivals):
        for h, (mask, last) in enumerate(pair):
            copy(h, mask - last, last).wait_recv()
            for step in orders[h][orders[h].index(last) + 1:]:
                c = copy(h, mask, step)
                c.start()
                sent.append(c)
    for c in sent:
        c.wait_send()
    own.wait()


def spread(n, table):
    return pl.pallas_call(
        functools.partial(spread_kernel, n),
        out_shape=jax.ShapeDtypeStruct((n,) + table.shape, jnp.int32),
        in_specs=[VMEM],
        out_specs=VMEM,
        scratch_shapes=[
            pltpu.SemaphoreType.DMA,
            pltpu.SemaphoreType.DMA((2, n)),
            pltpu.SemaphoreType.DMA((2, n)),
        ],
        compiler_params=pltpu.CompilerParams(collective_id=0, has_side_effects=True),
    )(table)


def scan(tab_ref, n, base, rows, keys):
    unit = min(8, rows)

    def tile(code, first, owner, acc):
        out = list(acc)
        for r in range(unit):
            words = jnp.broadcast_to(tab_ref[owner, pl.ds(first + r, 1), :], (8, LANES))
            for v, (high, lane) in enumerate(keys):
                got = jnp.take_along_axis(words, lane, axis=1, mode="promise_in_bounds")
                out[v] = jnp.where(high == code + r, got, out[v])
        return tuple(out)

    def per_owner(owner, acc):
        if rows == unit:
            return tile(owner * rows, base, owner, acc)
        return lax.fori_loop(
            0, rows // unit, lambda t, a: tile(owner * rows + t * unit, base + t * unit, owner, a), acc
        )

    zero = tuple(jnp.zeros((8, LANES), jnp.int32) for _ in keys)
    return list(lax.fori_loop(0, n, per_owner, zero))


def local_kernel(n, places, count_ref, date_ref, store_ref, product_ref, money_ref, tab_ref, o_ref,
                 word_buf, money_buf):
    tall = date_ref.shape[0]
    tiles = tall // 8
    (year_base, year_rows, year_words), (dflag_base, dflag_rows, dflag_words) = places[:2]
    (store_base, store_rows, store_words), (prod_base, prod_rows, prod_words) = places[2:4]
    brand_base, brand_rows, _ = places[4]

    def split(ref):
        return [ref[pl.ds(8 * v, 8), :] for v in range(tiles)]

    def keyed(word, per_shard, rows):
        owner, inside = word // per_shard, word % per_shard
        return owner * rows + inside // LANES, inside % LANES

    def where_is(keys, shift, words, rows):
        out = []
        for k in keys:
            w = lax.shift_right_logical(k, shift)
            owner = lax.shift_right_logical(w, words.bit_length() - 1)
            inside = w & (words - 1)
            out.append((owner * rows + lax.shift_right_logical(inside, 7), inside & (LANES - 1)))
        return out

    dates, stores, products = split(date_ref), split(store_ref), split(product_ref)
    year_word = scan(tab_ref, n, year_base, year_rows, where_is(dates, 3, year_words, year_rows))
    date_word = scan(tab_ref, n, dflag_base, dflag_rows, where_is(dates, 5, dflag_words, dflag_rows))
    store_word = scan(tab_ref, n, store_base, store_rows, where_is(stores, 5, store_words, store_rows))
    prod_word = scan(tab_ref, n, prod_base, prod_rows, where_is(products, 5, prod_words, prod_rows))
    count = count_ref[0]
    spot = lax.broadcasted_iota(jnp.int32, (8, LANES), 0) * LANES + lax.broadcasted_iota(
        jnp.int32, (8, LANES), 1
    )
    keep, packed = [], []
    for v in range(tiles):
        year = lax.shift_right_logical(year_word[v], (dates[v] & 7) * 4) & 15
        passed = lax.shift_right_logical(date_word[v], dates[v] & 31)
        passed &= lax.shift_right_logical(store_word[v], stores[v] & 31)
        passed &= lax.shift_right_logical(prod_word[v], products[v] & 31)
        passed &= 1
        keep.append(jnp.where(spot + v * 8 * LANES < count, passed, 0))
        packed.append(products[v] | (year << 20))
    keep = jnp.concatenate(keep, axis=0)
    packed = jnp.concatenate(packed, axis=0)
    row = lax.broadcasted_iota(jnp.int32, (tall, LANES), 0)

    upto = keep
    step = 1
    while step < tall:
        upto = upto + jnp.where(row >= step, pltpu.roll(upto, step, 0), 0)
        step *= 2
    most = jnp.max(upto[tall - 8:, :])
    word = jnp.where(keep == 1, packed | ((row - upto + 1) << 24), -1)
    money = jnp.where(keep == 1, money_ref[...], 0.0)
    step, bit = 1, 24
    while step < tall:
        far_word = pltpu.roll(word, tall - step, 0)
        far_money = pltpu.roll(money, tall - step, 0)
        comes = (far_word >= 0) & ((far_word & (1 << bit)) != 0)
        leaves = (word & (1 << bit)) != 0
        word = jnp.where(comes, far_word, jnp.where(leaves, -1, word))
        money = jnp.where(comes, far_money, jnp.where(leaves, 0.0, money))
        step *= 2
        bit += 1
    word_buf[...] = word
    money_buf[...] = money
    o_ref[...] = jnp.zeros_like(o_ref)

    shard_bits = (prod_words * 32).bit_length() - 1
    group_row = lax.broadcasted_iota(jnp.int32, (LANES, LANES), 0)

    def group(g, carry):
        keys, shifts, years = [], [], []
        for v in range(GROUP):
            w = word_buf[pl.ds(pl.multiple_of(g * GROUP * 8 + v * 8, 8), 8), :]
            key = w & 0xFFFFF
            owner = lax.shift_right_logical(key, shard_bits)
            inside = key & ((1 << shard_bits) - 1)
            third = ((inside.astype(jnp.float32) + 0.5) * (1.0 / 3.0)).astype(jnp.int32)
            shifts.append((inside - third * 3) * 10)
            keys.append((owner * brand_rows + lax.shift_right_logical(third, 7), third & (LANES - 1)))
            years.append(lax.shift_right_logical(w, 20) & 15)
        words = scan(tab_ref, n, brand_base, brand_rows, keys)
        total = o_ref[...]
        for v in range(GROUP):
            brand = lax.shift_right_logical(words[v], shifts[v]) & 1023
            high = lax.shift_right_logical(brand, 7) * YEARS + years[v]
            low = brand & (LANES - 1)
            cash = money_buf[pl.ds(pl.multiple_of(g * GROUP * 8 + v * 8, 8), 8), :]
            left, right = [], []
            for s in range(8):
                left.append(jnp.where(group_row == high[s:s + 1], cash[s:s + 1], 0.0).astype(jnp.bfloat16))
                right.append(jnp.where(group_row == low[s:s + 1], 1.0, 0.0).astype(jnp.bfloat16))
            total = total + lax.dot_general(
                jnp.concatenate(left, axis=1), jnp.concatenate(right, axis=1),
                (((1,), (1,)), ((), ())), preferred_element_type=jnp.float32,
            )
        o_ref[...] = total
        return carry

    lax.fori_loop(0, (most + GROUP * 8 - 1) // (GROUP * 8), group, 0)


def local(n, places, count, date, store, product, money, tables):
    tall = date.shape[0]
    return pl.pallas_call(
        functools.partial(local_kernel, n, places),
        out_shape=jax.ShapeDtypeStruct((LANES, LANES), jnp.float32),
        in_specs=[SMEM] + [VMEM] * 5,
        out_specs=VMEM,
        scratch_shapes=[pltpu.VMEM((tall, LANES), jnp.int32), pltpu.VMEM((tall, LANES), jnp.float32)],
    )(count, date, store, product, money, tables)


def join_kernel(nx, ny, x_ref, o_ref, in_x, part, in_y, whole, sx, rx, sy, ry, sz, rz):
    mx, my = lax.axis_index("gx"), lax.axis_index("gy")
    rows = part.shape[0]
    barrier = pltpu.get_barrier_semaphore()
    for d in range(1, nx):
        pl.semaphore_signal(barrier, inc=1, device_id={"gx": (mx + d) % nx}, device_id_type=MESH)
    for d in range(1, ny):
        pl.semaphore_signal(barrier, inc=1, device_id={"gy": (my + d) % ny}, device_id_type=MESH)
    pl.semaphore_wait(barrier, nx + ny - 2)

    def push(src, dst, send, recv, where):
        c = pltpu.make_async_remote_copy(
            src_ref=src, dst_ref=dst, send_sem=send, recv_sem=recv, device_id=where, device_id_type=MESH
        )
        c.start()
        return c

    first = []
    for d in range(1, nx):
        to = (mx + d) % nx
        first.append(push(x_ref.at[to], in_x.at[d - 1], sx.at[d - 1], rx.at[d - 1], {"gx": to}))
    total = x_ref[mx]
    for d, c in enumerate(first):
        c.wait_recv()
        total = total + in_x[d]
    part[...] = total
    second = []
    for d in range(1, ny):
        second.append(push(part, in_y.at[(my)], sy.at[d - 1], ry.at[d - 1], {"gy": (my + d) % ny}))
    for c in second:
        c.wait_recv()
    in_y[my] = total
    total = in_y[0]
    for d in range(1, ny):
        total = total + in_y[d]
    whole[mx] = total
    third = []
    for d in range(1, nx):
        third.append(push(whole.at[mx], whole.at[mx], sz.at[d - 1], rz.at[d - 1], {"gx": (mx + d) % nx}))
    for c in third:
        c.wait_recv()
    flat = whole[...].reshape(nx * rows, LANES)
    for j in range(BRANDS // LANES):
        o_ref[:, j * LANES:(j + 1) * LANES] = flat[j * YEARS:(j + 1) * YEARS]
    for c in first + second + third:
        c.wait_send()


def join(nx, ny, sums):
    rows = LANES // nx
    dma = pltpu.SemaphoreType.DMA
    return pl.pallas_call(
        functools.partial(join_kernel, nx, ny),
        out_shape=jax.ShapeDtypeStruct((YEARS, BRANDS), jnp.float32),
        in_specs=[VMEM],
        out_specs=VMEM,
        scratch_shapes=[
            pltpu.VMEM((nx - 1, rows, LANES), jnp.float32),
            pltpu.VMEM((rows, LANES), jnp.float32),
            pltpu.VMEM((ny, rows, LANES), jnp.float32),
            pltpu.VMEM((nx, rows, LANES), jnp.float32),
            dma((nx,)), dma((nx,)), dma((ny,)), dma((ny,)), dma((nx,)), dma((nx,)),
        ],
        compiler_params=pltpu.CompilerParams(collective_id=1, has_side_effects=True),
    )(sums.reshape(nx, rows, LANES))


def shards(nx, ny, date_key, store_key, product_key, revenue, row_counts,
           date_years, date_flags, store_flags, product_flags, brand_words):
    sections = [None] * 5
    pieces, base = [], 0
    tables = (date_years, date_flags, store_flags, product_flags, brand_words)
    for at in (4, 3, 2, 1, 0):
        words = tables[at].shape[0]
        rows = up(words, LANES) // LANES
        rows = up(rows, 8) if rows > 8 else rows
        sections[at] = (base, rows, words)
        pieces.append(jnp.pad(tables[at], (0, rows * LANES - words)))
        base += rows
    tail = up(base, 16) - base
    if tail:
        pieces.append(jnp.zeros((tail * LANES,), jnp.int32))
    table = jnp.concatenate(pieces).reshape(base + tail, LANES)
    tabs = spread(nx, table)
    flat = lambda a: a.reshape(-1, LANES)
    sums = local(nx, tuple(sections), row_counts, flat(date_key), flat(store_key), flat(product_key),
                 flat(revenue.astype(jnp.float32)), tabs)
    return join(nx, ny, sums)


def solution(mesh):
    rows = P(("gx", "gy"))
    return jax.shard_map(
        functools.partial(shards, mesh.shape["gx"], mesh.shape["gy"]),
        mesh=mesh,
        in_specs=(rows,) * 5 + (P("gx"),) * 5,
        out_specs=P(),
        check_vma=False,
    )
```

time: 649 us -> 108 us (0.17)
  waiting for transfers between devices: 446 us -> 0 us
  local copies, waits for them, and re-layouts: 151 us -> 5.82 us
  Pallas kernels: 0 us -> 100 us
  blocking collectives: 26.7 us -> 0 us
  between operations: 16.1 us -> 0.69 us
    psum x1 -> x0, waiting for transfers between devices: 414 us -> none  [shards(): result = lax.psum(group_sums, ('gx', 'gy'))]
    gather x5 -> x0, local copies, waits for them, and re-layouts: 145 us -> none  [the longest x3 73.6 us: pick_bits(): chosen = packed[position // per_word]]
    pallas_call x0 -> x3, Pallas kernels: none -> 100 us  [the longest x1 68.8 us: local(): pl.pallas_call(functools.partial(local_kernel, n, places), out_shape=jax....]
    unnamed x3 -> x0, waiting for transfers between devices: 32 us -> none
    all_gather x2 -> x0, blocking collectives: 17.1 us -> none  [the longest x1 8.95 us: shards(): lax.all_gather(product_flags, 'gx', axis=0, tiled=True)]
    unnamed x1 -> x0, blocking collectives: 9.58 us -> none
  transfers between devices with their start and end apart: 2 -> 0, of which waited for: 2 -> 0; matrix products, arithmetic and copies ran while one was open for 0% -> 0% of each run, Pallas kernels for 0% -> 0%
where the time goes in v1:
time: 108 us; the launch traced here: 107 us
  Pallas kernels  100 us (93%)
  local copies, waits for them, and re-layouts  5.82 us (5%)
    pallas_call x1, Pallas kernels, local(): pl.pallas_call(functools.partial(local_kernel, n, places), out_shape=jax....  68.8 us
    pallas_call x1, Pallas kernels, spread(): pl.pallas_call(functools.partial(spread_kernel, n), out_shape=jax.ShapeDt...  16.7 us
    pallas_call x1, Pallas kernels, join(): pl.pallas_call(functools.partial(join_kernel, nx, ny), out_shape=jax.Shap...  14.9 us
    unnamed x10, local copies, waits for them, and re-layouts  5.82 us

profile of v1, /device:TPU:0, one launch (start us, length us, event | category | flops | bytes accessed | tf_op | source)
XLA Modules:
  0.0 107.5 jit_solution(11034139842183158102)
XLA Ops:
  0.0 0.0 copy-start.1
  0.0 0.9 pad_dynamic-update-slice_fusion
  0.9 0.7 constant_dynamic-update-slice_fusion.4
  1.7 0.7 constant_dynamic-update-slice_fusion.3
  2.4 0.7 constant_dynamic-update-slice_fusion.2
  3.0 0.7 constant_dynamic-update-slice_fusion.1
  3.7 0.0 copy-start
  3.7 0.7 copy-done
  4.4 16.7 %shard_map.100.tab_ref = s32[8,384,128]{2,1,0:T(8,128)} custom-call(s32[384,128]{1,0:T(8,128)} %bitcast.8), custom_call_target="tpu_custom_call" | custom-call | tf_op jit(solution)/shard_map/pallas_call | solution.py:86
  21.1 0.0 copy-done.1
  21.1 0.6 bitcast_convert_fusion.money_ref
  22.3 68.8 %shard_map.101 = f32[128,128]{1,0:T(8,128)} custom-call(s32[1]{0:T(128)S(6)} %copy.17.count_ref, s32[96,128]{1,0:T(8,128)} %bitcast.10, s32[96,128]{1,0:T(8,128)} %bitcast.11, s32[96,128]{1,0:T(8,128)} %bitcast.12, f32[96,128]{1,0:T(8,128)} %bitcast_convert_fusion.money_ref, s32[8,384,128]{2,1,0:T(8,128)} %shard_map.100.tab_ref), custom_call_target="tpu_custom_call" | custom-call | tf_op jit(solution)/shard_map/pallas_call | solution.py:228
  91.1 14.9 %shard_map.102 = f32[16,1024]{1,0:T(8,128)} custom-call(f32[8,16,128]{2,1,0:T(8,128)} %bitcast.9), custom_call_target="tpu_custom_call" | custom-call | tf_op jit(solution)/shard_map/pallas_call | solution.py:288
  106.0 1.5 %copy.18 = f32[16,1024]{1,0:T(8,128)} copy(f32[16,1024]{1,0:T(8,128)} %shard_map.102) | data formatting | bytes 131072
  (1 shorter events, 0.0 us)
Async XLA Ops:
  0.0 21.1 %copy-start.1 = (bf16[12288]{0:T(1024)(128)(2,1)S(1)}, bf16[12288]{0:T(1024)(128)(2,1)}, u32[]{:S(2)}) copy-start(bf16[12288]{0:T(1024)(128)(2,1)} %param.13) | copy-start | bytes 73732
  3.7 0.7 copy-start

commit v2 on v1

--- a/solution.py
+++ b/solution.py
@@ -10,7 +10,6 @@
 BRANDS = 1024
 YEARS = 16
 LANES = 128
-GROUP = 4
 MESH = pl.DeviceIdType.MESH
 VMEM = pl.BlockSpec(memory_space=pltpu.VMEM)
 SMEM = pl.BlockSpec(memory_space=pltpu.SMEM)
@@ -97,27 +96,23 @@
     )(table)
 
 
-def scan(tab_ref, n, base, rows, keys):
-    unit = min(8, rows)
-
-    def tile(code, first, owner, acc):
-        out = list(acc)
-        for r in range(unit):
-            words = jnp.broadcast_to(tab_ref[owner, pl.ds(first + r, 1), :], (8, LANES))
-            for v, (high, lane) in enumerate(keys):
-                got = jnp.take_along_axis(words, lane, axis=1, mode="promise_in_bounds")
-                out[v] = jnp.where(high == code + r, got, out[v])
-        return tuple(out)
-
-    def per_owner(owner, acc):
-        if rows == unit:
-            return tile(owner * rows, base, owner, acc)
-        return lax.fori_loop(
-            0, rows // unit, lambda t, a: tile(owner * rows + t * unit, base + t * unit, owner, a), acc
-        )
-
-    zero = tuple(jnp.zeros((8, LANES), jnp.int32) for _ in keys)
-    return list(lax.fori_loop(0, n, per_owner, zero))
+DIMS = lax.GatherDimensionNumbers(
+    offset_dims=(), collapsed_slice_dims=(1,), start_index_map=(1,),
+    operand_batching_dims=(0,), start_indices_batching_dims=(0,),
+)
+
+
+def along_lanes(words, lane):
+    return lax.gather(words, lane[..., None], DIMS, (1, 1), mode=lax.GatherScatterMode.PROMISE_IN_BOUNDS)
+
+
+def pick(tab_ref, owner, base, rows, high, lane):
+    parts = [jnp.zeros((8, LANES), jnp.int32) for _ in range(4)]
+    mine = high - owner * rows
+    for r in range(rows):
+        words = jnp.broadcast_to(tab_ref[owner, pl.ds(base + r, 1), :], (8, LANES))
+        parts[r % 4] = jnp.where(mine == r, along_lanes(words, lane), parts[r % 4])
+    return (parts[0] | parts[1]) | (parts[2] | parts[3])
 
 
 def local_kernel(n, places, count_ref, date_ref, store_ref, product_ref, money_ref, tab_ref, o_ref,
@@ -128,42 +123,42 @@
     (store_base, store_rows, store_words), (prod_base, prod_rows, prod_words) = places[2:4]
     brand_base, brand_rows, _ = places[4]
 
-    def split(ref):
-        return [ref[pl.ds(8 * v, 8), :] for v in range(tiles)]
-
-    def keyed(word, per_shard, rows):
-        owner, inside = word // per_shard, word % per_shard
-        return owner * rows + inside // LANES, inside % LANES
-
-    def where_is(keys, shift, words, rows):
-        out = []
-        for k in keys:
-            w = lax.shift_right_logical(k, shift)
-            owner = lax.shift_right_logical(w, words.bit_length() - 1)
-            inside = w & (words - 1)
-            out.append((owner * rows + lax.shift_right_logical(inside, 7), inside & (LANES - 1)))
-        return out
-
-    dates, stores, products = split(date_ref), split(store_ref), split(product_ref)
-    year_word = scan(tab_ref, n, year_base, year_rows, where_is(dates, 3, year_words, year_rows))
-    date_word = scan(tab_ref, n, dflag_base, dflag_rows, where_is(dates, 5, dflag_words, dflag_rows))
-    store_word = scan(tab_ref, n, store_base, store_rows, where_is(stores, 5, store_words, store_rows))
-    prod_word = scan(tab_ref, n, prod_base, prod_rows, where_is(products, 5, prod_words, prod_rows))
+    def where_is(k, shift, words, rows):
+        w = lax.shift_right_logical(k, shift)
+        owner = lax.shift_right_logical(w, words.bit_length() - 1)
+        inside = w & (words - 1)
+        return owner * rows + lax.shift_right_logical(inside, 7), inside & (LANES - 1)
+
+    def look(keys, shift, base, rows, words):
+        high, lane = where_is(keys, shift, words, rows)
+        if n * rows <= 512:
+            out = jnp.zeros((8, LANES), jnp.int32)
+            for owner in range(n):
+                out = out | pick(tab_ref, owner, base, rows, high, lane)
+            return out
+        return lax.fori_loop(
+            0, n, lambda o, acc: acc | pick(tab_ref, o, base, rows, high, lane), jnp.zeros((8, LANES), jnp.int32)
+        )
+
     count = count_ref[0]
     spot = lax.broadcasted_iota(jnp.int32, (8, LANES), 0) * LANES + lax.broadcasted_iota(
         jnp.int32, (8, LANES), 1
     )
-    keep, packed = [], []
-    for v in range(tiles):
-        year = lax.shift_right_logical(year_word[v], (dates[v] & 7) * 4) & 15
-        passed = lax.shift_right_logical(date_word[v], dates[v] & 31)
-        passed &= lax.shift_right_logical(store_word[v], stores[v] & 31)
-        passed &= lax.shift_right_logical(prod_word[v], products[v] & 31)
-        passed &= 1
-        keep.append(jnp.where(spot + v * 8 * LANES < count, passed, 0))
-        packed.append(products[v] | (year << 20))
-    keep = jnp.concatenate(keep, axis=0)
-    packed = jnp.concatenate(packed, axis=0)
+
+    def filter_tile(v, carry):
+        at = pl.ds(pl.multiple_of(v * 8, 8), 8)
+        date, store, product = date_ref[at, :], store_ref[at, :], product_ref[at, :]
+        year = lax.shift_right_logical(look(date, 3, year_base, year_rows, year_words), (date & 7) * 4) & 15
+        passed = lax.shift_right_logical(look(date, 5, dflag_base, dflag_rows, dflag_words), date & 31)
+        passed &= lax.shift_right_logical(look(store, 5, store_base, store_rows, store_words), store & 31)
+        passed &= lax.shift_right_logical(look(product, 5, prod_base, prod_rows, prod_words), product & 31)
+        live = spot + v * (8 * LANES) < count
+        word_buf[at, :] = jnp.where(live & ((passed & 1) == 1), product | (year << 20), -1)
+        return carry
+
+    lax.fori_loop(0, tiles, filter_tile, 0)
+    packed = word_buf[...]
+    keep = (packed >= 0).astype(jnp.int32)
     row = lax.broadcasted_iota(jnp.int32, (tall, LANES), 0)
 
     upto = keep
@@ -192,35 +187,34 @@
     group_row = lax.broadcasted_iota(jnp.int32, (LANES, LANES), 0)
 
     def group(g, carry):
-        keys, shifts, years = [], [], []
-        for v in range(GROUP):
-            w = word_buf[pl.ds(pl.multiple_of(g * GROUP * 8 + v * 8, 8), 8), :]
-            key = w & 0xFFFFF
-            owner = lax.shift_right_logical(key, shard_bits)
-            inside = key & ((1 << shard_bits) - 1)
-            third = ((inside.astype(jnp.float32) + 0.5) * (1.0 / 3.0)).astype(jnp.int32)
-            shifts.append((inside - third * 3) * 10)
-            keys.append((owner * brand_rows + lax.shift_right_logical(third, 7), third & (LANES - 1)))
-            years.append(lax.shift_right_logical(w, 20) & 15)
-        words = scan(tab_ref, n, brand_base, brand_rows, keys)
-        total = o_ref[...]
-        for v in range(GROUP):
-            brand = lax.shift_right_logical(words[v], shifts[v]) & 1023
-            high = lax.shift_right_logical(brand, 7) * YEARS + years[v]
-            low = brand & (LANES - 1)
-            cash = money_buf[pl.ds(pl.multiple_of(g * GROUP * 8 + v * 8, 8), 8), :]
-            left, right = [], []
-            for s in range(8):
-                left.append(jnp.where(group_row == high[s:s + 1], cash[s:s + 1], 0.0).astype(jnp.bfloat16))
-                right.append(jnp.where(group_row == low[s:s + 1], 1.0, 0.0).astype(jnp.bfloat16))
-            total = total + lax.dot_general(
-                jnp.concatenate(left, axis=1), jnp.concatenate(right, axis=1),
-                (((1,), (1,)), ((), ())), preferred_element_type=jnp.float32,
-            )
-        o_ref[...] = total
+        at = pl.ds(pl.multiple_of(g * 8, 8), 8)
+        w = word_buf[at, :]
+        cash = money_buf[at, :]
+        key = w & 0xFFFFF
+        owner = lax.shift_right_logical(key, shard_bits)
+        inside = key & ((1 << shard_bits) - 1)
+        third = ((inside.astype(jnp.float32) + 0.5) * (1.0 / 3.0)).astype(jnp.int32)
+        shift = (inside - third * 3) * 10
+        high = owner * brand_rows + lax.shift_right_logical(third, 7)
+        lane = third & (LANES - 1)
+        words = lax.fori_loop(
+            0, n, lambda o, acc: acc | pick(tab_ref, o, brand_base, brand_rows, high, lane),
+            jnp.zeros((8, LANES), jnp.int32),
+        )
+        brand = lax.shift_right_logical(words, shift) & 1023
+        row_code = lax.shift_right_logical(brand, 7) * YEARS + (lax.shift_right_logical(w, 20) & 15)
+        low = brand & (LANES - 1)
+        left, right = [], []
+        for s in range(8):
+            left.append(jnp.where(group_row == row_code[s:s + 1], cash[s:s + 1], 0.0).astype(jnp.bfloat16))
+            right.append(jnp.where(group_row == low[s:s + 1], 1.0, 0.0).astype(jnp.bfloat16))
+        o_ref[...] += lax.dot_general(
+            jnp.concatenate(left, axis=1), jnp.concatenate(right, axis=1),
+            (((1,), (1,)), ((), ())), preferred_element_type=jnp.float32,
+        )
         return carry
 
-    lax.fori_loop(0, (most + GROUP * 8 - 1) // (GROUP * 8), group, 0)
+    lax.fori_loop(0, (most + 7) // 8, group, 0)
 
 
 def local(n, places, count, date, store, product, money, tables):
@@ -304,19 +298,20 @@
 def shards(nx, ny, date_key, store_key, product_key, revenue, row_counts,
            date_years, date_flags, store_flags, product_flags, brand_words):
     sections = [None] * 5
-    pieces, base = [], 0
+    base = 0
     tables = (date_years, date_flags, store_flags, product_flags, brand_words)
     for at in (4, 3, 2, 1, 0):
         words = tables[at].shape[0]
         rows = up(words, LANES) // LANES
         rows = up(rows, 8) if rows > 8 else rows
         sections[at] = (base, rows, words)
-        pieces.append(jnp.pad(tables[at], (0, rows * LANES - words)))
         base += rows
-    tail = up(base, 16) - base
-    if tail:
-        pieces.append(jnp.zeros((tail * LANES,), jnp.int32))
-    table = jnp.concatenate(pieces).reshape(base + tail, LANES)
+    tall = up(base, 16)
+    table = jnp.zeros((tall * LANES,), jnp.int32)
+    for at in range(5):
+        first, _, words = sections[at]
+        table = table | jnp.pad(tables[at], (first * LANES, (tall - first) * LANES - words))
+    table = table.reshape(tall, LANES)
     tabs = spread(nx, table)
     flat = lambda a: a.reshape(-1, LANES)
     sums = local(nx, tuple(sections), row_counts, flat(date_key), flat(store_key), flat(product_key),

time: 108 us -> 56.1 us (0.52)
  Pallas kernels: 100 us -> 51.3 us
  local copies, waits for them, and re-layouts: 5.82 us -> 1.48 us
  other arithmetic: 0.62 us -> 2.25 us
    pallas_call x1, Pallas kernels: 68.8 us -> 15.9 us  [local(): pl.pallas_call(functools.partial(local_kernel, n, places), out_shape=jax....]
    unnamed x10 -> x3, local copies, waits for them, and re-layouts: 5.82 us -> 1.48 us
    pallas_call x1, Pallas kernels: 14.9 us -> 18.7 us  [join(): pl.pallas_call(functools.partial(join_kernel, nx, ny), out_shape=jax.Shap...]
    reshape x0 -> x1, other arithmetic: none -> 1.64 us  [shards(): table = table.reshape(tall, LANES)]
where the time goes in v2:
time: 56.1 us; the launch traced here: 55.7 us
  Pallas kernels  51.3 us (91%)
  other arithmetic  2.25 us (4%)
  local copies, waits for them, and re-layouts  1.48 us (3%)
  between operations  0.68 us (1%)
    pallas_call x1, Pallas kernels, join(): pl.pallas_call(functools.partial(join_kernel, nx, ny), out_shape=jax.Shap...  18.7 us
    pallas_call x1, Pallas kernels, spread(): pl.pallas_call(functools.partial(spread_kernel, n), out_shape=jax.ShapeDt...  16.7 us
    pallas_call x1, Pallas kernels, local(): pl.pallas_call(functools.partial(local_kernel, n, places), out_shape=jax....  15.9 us
    reshape x1, other arithmetic, shards(): table = table.reshape(tall, LANES)  1.64 us
    unnamed x3, local copies, waits for them, and re-layouts  1.48 us

profile of v2, /device:TPU:0, one launch (start us, length us, event | category | flops | bytes accessed | tf_op | source)
XLA Modules:
  0.0 55.7 jit_solution(9633439676239394468)
XLA Ops:
  0.0 0.0 copy-start
  0.0 1.6 %or_bitcast_fusion.x_ref = s32[384,128]{1,0:T(8,128)} fusion(s32[43696]{0:T(1024)} %param.19, s32[4096]{0:T(1024)} %param.18, s32[256]{0:T(256)} %param.17, s32[16]{0:T(128)} %param.16, s32[64]{0:T(128)} %param.15), kind=kLoop, calls=%fused_computation | loop fusion | flops 196608 | bytes 389120 | tf_op jit(solution)/shard_map/reshape | solution.py:314
  1.6 16.7 %shard_map.100.tab_ref = s32[8,384,128]{2,1,0:T(8,128)} custom-call(s32[384,128]{1,0:T(8,128)} %or_bitcast_fusion.x_ref), custom_call_target="tpu_custom_call" | custom-call | tf_op jit(solution)/shard_map/pallas_call | solution.py:85
  18.3 0.0 copy-done
  18.3 0.6 %bitcast_convert_fusion.money_ref = f32[96,128]{1,0:T(8,128)} fusion(bf16[12288]{0:T(1024)(128)(2,1)S(1)} %copy-done), kind=kLoop, calls=%fused_computation.1 | loop fusion | flops 12288 | bytes 73728 | tf_op jit(solution)/shard_map/reshape | solution.py:316
  19.6 15.9 %shard_map.101 = f32[128,128]{1,0:T(8,128)} custom-call(s32[1]{0:T(128)S(6)} %copy.12.count_ref, s32[96,128]{1,0:T(8,128)} %bitcast.10, s32[96,128]{1,0:T(8,128)} %bitcast.11, s32[96,128]{1,0:T(8,128)} %bitcast.12, f32[96,128]{1,0:T(8,128)} %bitcast_convert_fusion.money_ref, s32[8,384,128]{2,1,0:T(8,128)} %shard_map.100.tab_ref), custom_call_target="tpu_custom_call" | custom-call | tf_op jit(solution)/shard_map/pallas_call | solution.py:222
  35.5 18.7 %shard_map.102 = f32[16,1024]{1,0:T(8,128)} custom-call(f32[8,16,128]{2,1,0:T(8,128)} %bitcast.9), custom_call_target="tpu_custom_call" | custom-call | tf_op jit(solution)/shard_map/pallas_call | solution.py:282
  54.2 1.5 %copy.13 = f32[16,1024]{1,0:T(8,128)} copy(f32[16,1024]{1,0:T(8,128)} %shard_map.102) | data formatting | bytes 131072
Async XLA Ops:
  0.0 18.3 %copy-start = (bf16[12288]{0:T(1024)(128)(2,1)S(1)}, bf16[12288]{0:T(1024)(128)(2,1)}, u32[]{:S(2)}) copy-start(bf16[12288]{0:T(1024)(128)(2,1)} %param.13) | copy-start | bytes 73732

commit v3 on v2

--- a/solution.py
+++ b/solution.py
@@ -10,6 +10,7 @@
 BRANDS = 1024
 YEARS = 16
 LANES = 128
+CHAINS = 2
 MESH = pl.DeviceIdType.MESH
 VMEM = pl.BlockSpec(memory_space=pltpu.VMEM)
 SMEM = pl.BlockSpec(memory_space=pltpu.SMEM)
@@ -107,21 +108,34 @@
 
 
 def pick(tab_ref, owner, base, rows, high, lane):
-    parts = [jnp.zeros((8, LANES), jnp.int32) for _ in range(4)]
+    lots = min(CHAINS, rows)
+    parts = [jnp.zeros((8, LANES), jnp.int32) for _ in range(lots)]
     mine = high - owner * rows
     for r in range(rows):
         words = jnp.broadcast_to(tab_ref[owner, pl.ds(base + r, 1), :], (8, LANES))
-        parts[r % 4] = jnp.where(mine == r, along_lanes(words, lane), parts[r % 4])
-    return (parts[0] | parts[1]) | (parts[2] | parts[3])
-
-
-def local_kernel(n, places, count_ref, date_ref, store_ref, product_ref, money_ref, tab_ref, o_ref,
-                 word_buf, money_buf):
+        parts[r % lots] = jnp.where(mine == r, along_lanes(words, lane), parts[r % lots])
+    while len(parts) > 1:
+        parts = [a | b for a, b in zip(parts[::2], parts[1::2])] + parts[len(parts) // 2 * 2:]
+    return parts[0]
+
+
+def local_kernel(n, places, count_ref, date_ref, store_ref, product_ref, money_ref, all_ref, o_ref,
+                 word_buf, money_buf, tab_ref, sems):
     tall = date_ref.shape[0]
     tiles = tall // 8
     (year_base, year_rows, year_words), (dflag_base, dflag_rows, dflag_words) = places[:2]
     (store_base, store_rows, store_words), (prod_base, prod_rows, prod_words) = places[2:4]
     brand_base, brand_rows, _ = places[4]
+
+    small = pl.ds(prod_base, all_ref.shape[1] - prod_base)
+    large = pl.ds(0, prod_base)
+    fetches = [
+        pltpu.make_async_copy(all_ref.at[:, part], tab_ref.at[:, part], sems.at[k])
+        for k, part in enumerate((small, large))
+    ]
+    for f in fetches:
+        f.start()
+    fetches[0].wait()
 
     def where_is(k, shift, words, rows):
         w = lax.shift_right_logical(k, shift)
@@ -145,7 +159,7 @@
         jnp.int32, (8, LANES), 1
     )
 
-    def filter_tile(v, carry):
+    def filter_one(v):
         at = pl.ds(pl.multiple_of(v * 8, 8), 8)
         date, store, product = date_ref[at, :], store_ref[at, :], product_ref[at, :]
         year = lax.shift_right_logical(look(date, 3, year_base, year_rows, year_words), (date & 7) * 4) & 15
@@ -154,10 +168,16 @@
         passed &= lax.shift_right_logical(look(product, 5, prod_base, prod_rows, prod_words), product & 31)
         live = spot + v * (8 * LANES) < count
         word_buf[at, :] = jnp.where(live & ((passed & 1) == 1), product | (year << 20), -1)
+
+    both = 2 if tiles % 2 == 0 else 1
+
+    def filter_tiles(v, carry):
+        for k in range(both):
+            filter_one(v * both + k)
         return carry
 
-    lax.fori_loop(0, tiles, filter_tile, 0)
-    packed = word_buf[...]
+    lax.fori_loop(0, tiles // both, filter_tiles, 0)
+    packed = word_buf[pl.ds(0, tall), :]
     keep = (packed >= 0).astype(jnp.int32)
     row = lax.broadcasted_iota(jnp.int32, (tall, LANES), 0)
 
@@ -166,7 +186,9 @@
     while step < tall:
         upto = upto + jnp.where(row >= step, pltpu.roll(upto, step, 0), 0)
         step *= 2
-    most = jnp.max(upto[tall - 8:, :])
+    last = upto[tall - 8:, :]
+    most = jnp.max(last + pltpu.roll(last, LANES // 2, 1))
+    turns = (most + 15) // 16
     word = jnp.where(keep == 1, packed | ((row - upto + 1) << 24), -1)
     money = jnp.where(keep == 1, money_ref[...], 0.0)
     step, bit = 1, 24
@@ -179,17 +201,32 @@
         money = jnp.where(comes, far_money, jnp.where(leaves, 0.0, money))
         step *= 2
         bit += 1
-    word_buf[...] = word
-    money_buf[...] = money
+    word_buf[pl.ds(0, tall), :] = word
+    money_buf[pl.ds(0, tall), :] = money
+    word_buf[pl.ds(tall, 8), :] = jnp.full((8, LANES), -1, jnp.int32)
+    money_buf[pl.ds(tall, 8), :] = jnp.zeros((8, LANES), jnp.float32)
     o_ref[...] = jnp.zeros_like(o_ref)
+    fetches[1].wait()
 
     shard_bits = (prod_words * 32).bit_length() - 1
     group_row = lax.broadcasted_iota(jnp.int32, (LANES, LANES), 0)
 
+    few = min(4, n)
+    sub = lax.broadcasted_iota(jnp.int32, (8, LANES), 0)
+
+    def mirror(x):
+        x = pltpu.roll(x, LANES // 2, 1)
+        for step in (1, 2, 4):
+            x = jnp.where((sub & step) == 0, pltpu.roll(x, 8 - step, 0), pltpu.roll(x, step, 0))
+        return x
+
     def group(g, carry):
         at = pl.ds(pl.multiple_of(g * 8, 8), 8)
-        w = word_buf[at, :]
-        cash = money_buf[at, :]
+        over = pl.ds(pl.multiple_of(jnp.minimum(2 * turns - 1 - g, tiles) * 8, 8), 8)
+        w, cash = word_buf[at, :], money_buf[at, :]
+        spare = w < 0
+        w = jnp.where(spare, mirror(word_buf[over, :]), w)
+        cash = jnp.where(spare, mirror(money_buf[over, :]), cash)
         key = w & 0xFFFFF
         owner = lax.shift_right_logical(key, shard_bits)
         inside = key & ((1 << shard_bits) - 1)
@@ -197,10 +234,13 @@
         shift = (inside - third * 3) * 10
         high = owner * brand_rows + lax.shift_right_logical(third, 7)
         lane = third & (LANES - 1)
-        words = lax.fori_loop(
-            0, n, lambda o, acc: acc | pick(tab_ref, o, brand_base, brand_rows, high, lane),
-            jnp.zeros((8, LANES), jnp.int32),
-        )
+
+        def owners(t, acc):
+            for k in range(few):
+                acc = acc | pick(tab_ref, t * few + k, brand_base, brand_rows, high, lane)
+            return acc
+
+        words = lax.fori_loop(0, n // few, owners, jnp.zeros((8, LANES), jnp.int32))
         brand = lax.shift_right_logical(words, shift) & 1023
         row_code = lax.shift_right_logical(brand, 7) * YEARS + (lax.shift_right_logical(w, 20) & 15)
         low = brand & (LANES - 1)
@@ -214,7 +254,7 @@
         )
         return carry
 
-    lax.fori_loop(0, (most + 7) // 8, group, 0)
+    lax.fori_loop(0, turns, group, 0)
 
 
 def local(n, places, count, date, store, product, money, tables):
@@ -222,9 +262,10 @@
     return pl.pallas_call(
         functools.partial(local_kernel, n, places),
         out_shape=jax.ShapeDtypeStruct((LANES, LANES), jnp.float32),
-        in_specs=[SMEM] + [VMEM] * 5,
+        in_specs=[SMEM] + [VMEM] * 4 + [pl.BlockSpec(memory_space=pl.ANY)],
         out_specs=VMEM,
-        scratch_shapes=[pltpu.VMEM((tall, LANES), jnp.int32), pltpu.VMEM((tall, LANES), jnp.float32)],
+        scratch_shapes=[pltpu.VMEM((tall + 8, LANES), jnp.int32), pltpu.VMEM((tall + 8, LANES), jnp.float32),
+            pltpu.VMEM(tables.shape, jnp.int32), pltpu.SemaphoreType.DMA((2,))],
     )(count, date, store, product, money, tables)
 
 

time: 56.1 us -> 54.6 us (0.973)
  Pallas kernels: 51.3 us -> 49.9 us
    pallas_call x1, Pallas kernels: 15.9 us -> 14.8 us  [local(): pl.pallas_call(functools.partial(local_kernel, n, places), out_shape=jax....]
where the time goes in v3:
time: 54.6 us; the launch traced here: 54.3 us
  Pallas kernels  49.9 us (91%)
  other arithmetic  2.25 us (4%)
  local copies, waits for them, and re-layouts  1.48 us (3%)
  between operations  0.69 us (1%)
    pallas_call x1, Pallas kernels, join(): pl.pallas_call(functools.partial(join_kernel, nx, ny), out_shape=jax.Shap...  18.4 us
    pallas_call x1, Pallas kernels, spread(): pl.pallas_call(functools.partial(spread_kernel, n), out_shape=jax.ShapeDt...  16.7 us
    pallas_call x1, Pallas kernels, local(): pl.pallas_call(functools.partial(local_kernel, n, places), out_shape=jax....  14.8 us
    reshape x1, other arithmetic, shards(): table = table.reshape(tall, LANES)  1.64 us
    unnamed x3, local copies, waits for them, and re-layouts  1.48 us

profile of v3, /device:TPU:0, one launch (start us, length us, event | category | flops | bytes accessed | tf_op | source)
XLA Modules:
  0.0 54.3 jit_solution(10534332317903817583)
XLA Ops:
  0.0 0.0 copy-start
  0.0 1.6 %or_bitcast_fusion.x_ref = s32[384,128]{1,0:T(8,128)} fusion(s32[43696]{0:T(1024)} %param.19, s32[4096]{0:T(1024)} %param.18, s32[256]{0:T(256)} %param.17, s32[16]{0:T(128)} %param.16, s32[64]{0:T(128)} %param.15), kind=kLoop, calls=%fused_computation | loop fusion | flops 196608 | bytes 389120 | tf_op jit(solution)/shard_map/reshape | solution.py:355
  1.6 16.7 %shard_map.100.all_ref = s32[8,384,128]{2,1,0:T(8,128)} custom-call(s32[384,128]{1,0:T(8,128)} %or_bitcast_fusion.x_ref), custom_call_target="tpu_custom_call" | custom-call | tf_op jit(solution)/shard_map/pallas_call | solution.py:86
  18.3 0.0 copy-done
  18.3 0.6 %bitcast_convert_fusion.money_ref = f32[96,128]{1,0:T(8,128)} fusion(bf16[12288]{0:T(1024)(128)(2,1)S(1)} %copy-done), kind=kLoop, calls=%fused_computation.1 | loop fusion | flops 12288 | bytes 73728 | tf_op jit(solution)/shard_map/reshape | solution.py:357
  19.6 14.8 %shard_map.101 = f32[128,128]{1,0:T(8,128)} custom-call(s32[1]{0:T(128)S(6)} %copy.12.count_ref, s32[96,128]{1,0:T(8,128)} %bitcast.10, s32[96,128]{1,0:T(8,128)} %bitcast.11, s32[96,128]{1,0:T(8,128)} %bitcast.12, f32[96,128]{1,0:T(8,128)} %bitcast_convert_fusion.money_ref, s32[8,384,128]{2,1,0:T(8,128)} %shard_map.100.all_ref), custom_call_target="tpu_custom_call" | custom-call | tf_op jit(solution)/shard_map/pallas_call | solution.py:262
  34.4 18.4 %shard_map.102 = f32[16,1024]{1,0:T(8,128)} custom-call(f32[8,16,128]{2,1,0:T(8,128)} %bitcast.9), custom_call_target="tpu_custom_call" | custom-call | tf_op jit(solution)/shard_map/pallas_call | solution.py:323
  52.9 1.5 %copy.13 = f32[16,1024]{1,0:T(8,128)} copy(f32[16,1024]{1,0:T(8,128)} %shard_map.102) | data formatting | bytes 131072
Async XLA Ops:
  0.0 18.3 %copy-start = (bf16[12288]{0:T(1024)(128)(2,1)S(1)}, bf16[12288]{0:T(1024)(128)(2,1)}, u32[]{:S(2)}) copy-start(bf16[12288]{0:T(1024)(128)(2,1)} %param.13) | copy-start | bytes 73732

commit v4 on v3

--- a/solution.py
+++ b/solution.py
@@ -27,74 +27,6 @@
             out = out + bit * (1 - 2 * ((me // bit) % 2))
         bit *= 2
     return out
-
-
-def spread_kernel(n, x_ref, o_ref, own_sem, send_sem, recv_sem):
-    me = lax.axis_index("gx")
-    half = x_ref.shape[0] // 2
-    bits = n.bit_length() - 1
-    rising = [1 << b for b in range(1, bits)]
-    orders = (rising + [1], rising[::-1] + [1])
-    barrier = pltpu.get_barrier_semaphore()
-    for b in range(bits):
-        pl.semaphore_signal(barrier, inc=1, device_id={"gx": flip(me, 1 << b)}, device_id_type=MESH)
-    own = pltpu.make_async_copy(x_ref, o_ref.at[me], own_sem)
-    own.start()
-    pl.semaphore_wait(barrier, bits)
-
-    def copy(h, mask, step):
-        rows = pl.ds(h * half, half)
-        slot = flip(me, mask)
-        src = x_ref.at[rows] if mask == 0 else o_ref.at[slot, rows]
-        return pltpu.make_async_remote_copy(
-            src_ref=src,
-            dst_ref=o_ref.at[slot, rows],
-            send_sem=send_sem.at[h, mask + step],
-            recv_sem=recv_sem.at[h, mask + step],
-            device_id={"gx": flip(me, step)},
-            device_id_type=MESH,
-        )
-
-    sent = []
-    for h in range(2):
-        for step in orders[h]:
-            c = copy(h, 0, step)
-            c.start()
-            sent.append(c)
-    arrivals = []
-    for h in range(2):
-        have = [0]
-        listed = []
-        for step in orders[h]:
-            fresh = [m + step for m in have]
-            listed += [(m, step) for m in fresh]
-            have += fresh
-        arrivals.append(listed)
-    for pair in zip(*arrivals):
-        for h, (mask, last) in enumerate(pair):
-            copy(h, mask - last, last).wait_recv()
-            for step in orders[h][orders[h].index(last) + 1:]:
-                c = copy(h, mask, step)
-                c.start()
-                sent.append(c)
-    for c in sent:
-        c.wait_send()
-    own.wait()
-
-
-def spread(n, table):
-    return pl.pallas_call(
-        functools.partial(spread_kernel, n),
-        out_shape=jax.ShapeDtypeStruct((n,) + table.shape, jnp.int32),
-        in_specs=[VMEM],
-        out_specs=VMEM,
-        scratch_shapes=[
-            pltpu.SemaphoreType.DMA,
-            pltpu.SemaphoreType.DMA((2, n)),
-            pltpu.SemaphoreType.DMA((2, n)),
-        ],
-        compiler_params=pltpu.CompilerParams(collective_id=0, has_side_effects=True),
-    )(table)
 
 
 DIMS = lax.GatherDimensionNumbers(
@@ -119,23 +51,11 @@
     return parts[0]
 
 
-def local_kernel(n, places, count_ref, date_ref, store_ref, product_ref, money_ref, all_ref, o_ref,
-                 word_buf, money_buf, tab_ref, sems):
-    tall = date_ref.shape[0]
-    tiles = tall // 8
+def filter_rows(n, places, count_ref, date_ref, store_ref, product_ref, near, word_ref):
+    top = places[3][0]
+    tiles = date_ref.shape[0] // 8
     (year_base, year_rows, year_words), (dflag_base, dflag_rows, dflag_words) = places[:2]
     (store_base, store_rows, store_words), (prod_base, prod_rows, prod_words) = places[2:4]
-    brand_base, brand_rows, _ = places[4]
-
-    small = pl.ds(prod_base, all_ref.shape[1] - prod_base)
-    large = pl.ds(0, prod_base)
-    fetches = [
-        pltpu.make_async_copy(all_ref.at[:, part], tab_ref.at[:, part], sems.at[k])
-        for k, part in enumerate((small, large))
-    ]
-    for f in fetches:
-        f.start()
-    fetches[0].wait()
 
     def where_is(k, shift, words, rows):
         w = lax.shift_right_logical(k, shift)
@@ -148,10 +68,10 @@
         if n * rows <= 512:
             out = jnp.zeros((8, LANES), jnp.int32)
             for owner in range(n):
-                out = out | pick(tab_ref, owner, base, rows, high, lane)
+                out = out | pick(near, owner, base - top, rows, high, lane)
             return out
         return lax.fori_loop(
-            0, n, lambda o, acc: acc | pick(tab_ref, o, base, rows, high, lane), jnp.zeros((8, LANES), jnp.int32)
+            0, n, lambda o, acc: acc | pick(near, o, base - top, rows, high, lane), jnp.zeros((8, LANES), jnp.int32)
         )
 
     count = count_ref[0]
@@ -167,7 +87,7 @@
         passed &= lax.shift_right_logical(look(store, 5, store_base, store_rows, store_words), store & 31)
         passed &= lax.shift_right_logical(look(product, 5, prod_base, prod_rows, prod_words), product & 31)
         live = spot + v * (8 * LANES) < count
-        word_buf[at, :] = jnp.where(live & ((passed & 1) == 1), product | (year << 20), -1)
+        word_ref[at, :] = jnp.where(live & ((passed & 1) == 1), product | (year << 20), -1)
 
     both = 2 if tiles % 2 == 0 else 1
 
@@ -177,7 +97,109 @@
         return carry
 
     lax.fori_loop(0, tiles // both, filter_tiles, 0)
-    packed = word_buf[pl.ds(0, tall), :]
+
+
+def spread_kernel(n, places, count_ref, date_ref, store_ref, product_ref, x_ref, o_ref, word_ref,
+                  near, own_sem, send_sem, recv_sem):
+    me = lax.axis_index("gx")
+    top = o_ref.shape[1]
+    cut = top // 16 * 8
+    spans = ((top, near.shape[1], near), (0, cut, o_ref), (cut, top - cut, o_ref))
+    bits = n.bit_length() - 1
+    rising = [1 << b for b in range(1, bits)]
+    orders = (rising + [1], rising + [1], rising[::-1] + [1])
+    barrier = pltpu.get_barrier_semaphore()
+    for b in range(bits):
+        pl.semaphore_signal(barrier, inc=1, device_id={"gx": flip(me, 1 << b)}, device_id_type=MESH)
+    owns = []
+    for k, (first, rows, ref) in enumerate(((top, near.shape[1], near), (0, top, o_ref))):
+        own = pltpu.make_async_copy(x_ref.at[pl.ds(first, rows)], ref.at[me], own_sem.at[k])
+        own.start()
+        owns.append(own)
+    pl.semaphore_wait(barrier, bits)
+
+    def copy(h, mask, step):
+        first, rows, ref = spans[h]
+        slot = flip(me, mask)
+        dst = ref.at[slot] if h == 0 else ref.at[slot, pl.ds(first, rows)]
+        return pltpu.make_async_remote_copy(
+            src_ref=x_ref.at[pl.ds(first, rows)] if mask == 0 else dst,
+            dst_ref=dst,
+            send_sem=send_sem.at[h, mask + step],
+            recv_sem=recv_sem.at[h, mask + step],
+            device_id={"gx": flip(me, step)},
+            device_id_type=MESH,
+        )
+
+    sent = []
+    for h in range(3):
+        for step in orders[h]:
+            c = copy(h, 0, step)
+            c.start()
+            sent.append(c)
+    arrivals = []
+    for h in range(3):
+        have = [0]
+        listed = []
+        for step in orders[h]:
+            fresh = [m + step for m in have]
+            listed += [(m, step) for m in fresh]
+            have += fresh
+        arrivals.append(listed)
+
+    def arrive(h, mask, last):
+        copy(h, mask - last, last).wait_recv()
+        for step in orders[h][orders[h].index(last) + 1:]:
+            c = copy(h, mask, step)
+            c.start()
+            sent.append(c)
+
+    for mask, last in arrivals[0][:n // 2 - 1]:
+        arrive(0, mask, last)
+    early = 1 if n > 2 else 0
+    for k in range(early):
+        for h in (1, 2):
+            arrive(h, *arrivals[h][k])
+    for mask, last in arrivals[0][n // 2 - 1:]:
+        arrive(0, mask, last)
+    owns[0].wait()
+    filter_rows(n, places, count_ref, date_ref, store_ref, product_ref, near, word_ref)
+    for k in range(early, n - 1):
+        for h in (1, 2):
+            arrive(h, *arrivals[h][k])
+    for c in sent:
+        c.wait_send()
+    owns[1].wait()
+
+
+def spread(n, places, count, date, store, product, table):
+    top, low = places[3][0], table.shape[0] - places[3][0]
+    return pl.pallas_call(
+        functools.partial(spread_kernel, n, places),
+        out_shape=(
+            jax.ShapeDtypeStruct((n, top, LANES), jnp.int32),
+            jax.ShapeDtypeStruct(date.shape, jnp.int32),
+        ),
+        in_specs=[SMEM] + [VMEM] * 4,
+        out_specs=(VMEM, VMEM),
+        scratch_shapes=[
+            pltpu.VMEM((n, low, LANES), jnp.int32),
+            pltpu.SemaphoreType.DMA((2,)),
+            pltpu.SemaphoreType.DMA((3, n)),
+            pltpu.SemaphoreType.DMA((3, n)),
+        ],
+        compiler_params=pltpu.CompilerParams(collective_id=0, has_side_effects=True),
+    )(count, date, store, product, table)
+
+
+def local_kernel(n, places, packed_ref, money_ref, all_ref, o_ref, word_buf, money_buf, tab_ref, sem):
+    tall = packed_ref.shape[0]
+    tiles = tall // 8
+    prod_words = places[3][2]
+    brand_base, brand_rows, _ = places[4]
+    fetch = pltpu.make_async_copy(all_ref, tab_ref, sem)
+    fetch.start()
+    packed = packed_ref[...]
     keep = (packed >= 0).astype(jnp.int32)
     row = lax.broadcasted_iota(jnp.int32, (tall, LANES), 0)
 
@@ -206,7 +228,7 @@
     word_buf[pl.ds(tall, 8), :] = jnp.full((8, LANES), -1, jnp.int32)
     money_buf[pl.ds(tall, 8), :] = jnp.zeros((8, LANES), jnp.float32)
     o_ref[...] = jnp.zeros_like(o_ref)
-    fetches[1].wait()
+    fetch.wait()
 
     shard_bits = (prod_words * 32).bit_length() - 1
     group_row = lax.broadcasted_iota(jnp.int32, (LANES, LANES), 0)
@@ -257,16 +279,18 @@
     lax.fori_loop(0, turns, group, 0)
 
 
-def local(n, places, count, date, store, product, money, tables):
-    tall = date.shape[0]
+def local(n, places, packed, money, tables):
+    tall = packed.shape[0]
     return pl.pallas_call(
         functools.partial(local_kernel, n, places),
         out_shape=jax.ShapeDtypeStruct((LANES, LANES), jnp.float32),
-        in_specs=[SMEM] + [VMEM] * 4 + [pl.BlockSpec(memory_space=pl.ANY)],
+        in_specs=[VMEM, VMEM, pl.BlockSpec(memory_space=pl.ANY)],
         out_specs=VMEM,
-        scratch_shapes=[pltpu.VMEM((tall + 8, LANES), jnp.int32), pltpu.VMEM((tall + 8, LANES), jnp.float32),
-            pltpu.VMEM(tables.shape, jnp.int32), pltpu.SemaphoreType.DMA((2,))],
-    )(count, date, store, product, money, tables)
+        scratch_shapes=[
+            pltpu.VMEM((tall + 8, LANES), jnp.int32), pltpu.VMEM((tall + 8, LANES), jnp.float32),
+            pltpu.VMEM(tables.shape, jnp.int32), pltpu.SemaphoreType.DMA,
+        ],
+    )(packed, money, tables)
 
 
 def join_kernel(nx, ny, x_ref, o_ref, in_x, part, in_y, whole, sx, rx, sy, ry, sz, rz):
@@ -353,10 +377,10 @@
         first, _, words = sections[at]
         table = table | jnp.pad(tables[at], (first * LANES, (tall - first) * LANES - words))
     table = table.reshape(tall, LANES)
-    tabs = spread(nx, table)
+    places = tuple(sections)
     flat = lambda a: a.reshape(-1, LANES)
-    sums = local(nx, tuple(sections), row_counts, flat(date_key), flat(store_key), flat(product_key),
-                 flat(revenue.astype(jnp.float32)), tabs)
+    tabs, packed = spread(nx, places, row_counts, flat(date_key), flat(store_key), flat(product_key), table)
+    sums = local(nx, places, packed, flat(revenue.astype(jnp.float32)), tabs)
     return join(nx, ny, sums)
 
 

time: 54.6 us -> 52.8 us (0.967)
  Pallas kernels: 49.9 us -> 47.8 us
  other arithmetic: 2.25 us -> 2.97 us
    pallas_call x1, Pallas kernels: 14.8 us -> 9.84 us  [local(): pl.pallas_call(functools.partial(local_kernel, n, places), out_shape=jax....]
    pallas_call x1, Pallas kernels: 16.7 us -> 19.5 us  [spread(): pl.pallas_call(functools.partial(spread_kernel, n, places), out_shape=(ja...]
    reshape x1, other arithmetic: 0.62 us -> 1.35 us  [shards(): flat = lambda a: a.reshape(-1, LANES)]
    unnamed x3 -> x1, local copies, waits for them, and re-layouts: 1.48 us -> 1.47 us
where the time goes in v4:
time: 52.8 us; the launch traced here: 52.9 us
  Pallas kernels  47.8 us (91%)
  other arithmetic  2.97 us (6%)
  local copies, waits for them, and re-layouts  1.47 us (3%)
  between operations  0.68 us (1%)
    pallas_call x1, Pallas kernels, spread(): pl.pallas_call(functools.partial(spread_kernel, n, places), out_shape=(ja...  19.5 us
    pallas_call x1, Pallas kernels, join(): pl.pallas_call(functools.partial(join_kernel, nx, ny), out_shape=jax.Shap...  18.4 us
    pallas_call x1, Pallas kernels, local(): pl.pallas_call(functools.partial(local_kernel, n, places), out_shape=jax....  9.84 us
    reshape x1, other arithmetic, shards(): table = table.reshape(tall, LANES)  1.62 us
    unnamed x1, local copies, waits for them, and re-layouts  1.47 us
    reshape x1, other arithmetic, shards(): flat = lambda a: a.reshape(-1, LANES)  1.35 us

profile of v4, /device:TPU:0, one launch (start us, length us, event | category | flops | bytes accessed | tf_op | source)
XLA Modules:
  0.0 52.9 jit_solution(2673533641269935478)
XLA Ops:
  0.0 1.6 %or_bitcast_fusion.x_ref = s32[384,128]{1,0:T(8,128)} fusion(s32[43696]{0:T(1024)} %param.19, s32[4096]{0:T(1024)} %param.18, s32[256]{0:T(256)} %param.17, s32[16]{0:T(128)} %param.16, s32[64]{0:T(128)} %param.15), kind=kLoop, calls=%fused_computation | loop fusion | flops 196608 | bytes 389120 | tf_op jit(solution)/shard_map/reshape | solution.py:379
  2.3 19.5 %shard_map.100 = (s32[8,344,128]{2,1,0:T(8,128)}, s32[96,128]{1,0:T(8,128)}) custom-call(s32[1]{0:T(128)S(6)} %copy.12.count_ref, s32[96,128]{1,0:T(8,128)} %bitcast.10, s32[96,128]{1,0:T(8,128)} %bitcast.11, s32[96,128]{1,0:T(8,128)} %bitcast.12, s32[384,128]{1,0:T(8,128)} %or_bitcast_fusion.x_ref), custom_call_target="tpu_custom_call" | custom-call | tf_op jit(solution)/shard_map/pallas_call | solution.py:177
  21.8 1.4 %bitcast_convert_fusion.money_ref = f32[96,128]{1,0:T(8,128)} fusion(bf16[12288]{0:T(1024)(128)(2,1)} %param.13), kind=kLoop, calls=%fused_computation.1 | loop fusion | flops 12288 | bytes 73728 | tf_op jit(solution)/shard_map/reshape | solution.py:381
  23.2 9.8 %shard_map.101 = f32[128,128]{1,0:T(8,128)} custom-call(s32[96,128]{1,0:T(8,128)} %get-tuple-element.7.packed_ref, f32[96,128]{1,0:T(8,128)} %bitcast_convert_fusion.money_ref, s32[8,344,128]{2,1,0:T(8,128)} %get-tuple-element.8.all_ref), custom_call_target="tpu_custom_call" | custom-call | tf_op jit(solution)/shard_map/pallas_call | solution.py:284
  33.0 18.4 %shard_map.102 = f32[16,1024]{1,0:T(8,128)} custom-call(f32[8,16,128]{2,1,0:T(8,128)} %bitcast.9), custom_call_target="tpu_custom_call" | custom-call | tf_op jit(solution)/shard_map/pallas_call | solution.py:347
  51.5 1.5 %copy.13 = f32[16,1024]{1,0:T(8,128)} copy(f32[16,1024]{1,0:T(8,128)} %shard_map.102) | data formatting | bytes 131072
